TPU v7x, 32 devices: a whole 2x2x4 slice. The times are simulated.
32 devices in a mesh: row: 8 (over z, x), col: 4 (over y, core).
Axes of the slice: x: 2, y: 2, z: 4, core: 2. Of those that a mesh axis runs over, the one named last changes fastest.
Arguments:
- matrix: float32 [64, 8, 128, 128], P('row', 'col'), may hold values from -0.1875 to 0.1875
- columns: int32 [64, 8], P('row', 'col'), may hold values from 0 to 15
- counts: int32 [64, 4], P('row', 'col'), may hold values from 1 to 2
- fine_guess: float32 [64, 32, 128], P(('col', 'row')), may hold values from -6 to 6
- right_side: float32 [64, 32, 128], P(('row', 'col')), may hold values from -6 to 6
- aggregate: int32 [64], P(('row', 'col')), may hold values from 0 to 7
- restrict: float32 [64, 128, 128], P(('row', 'col')), may hold values from -0.5 to 0.5
Outputs:
- coarse_scaled: float32 [64, 32, 128], P('row')
- residual: float32 [64, 32, 128], P(('row', 'col'))
Inputs may be any that keep to these rules, and one draw needn't show every extreme that they name: `counts`: slots at or past the count hold no part of the operator.
All inputs are finite; a program needn't handle non-finite values.
Results may differ from a plain program's by a relative error of at most 0.000071.
Values sent between devices are 32-bit elements; how exact they have to be, the bound alone decides.
A program may use at most 64 MiB of HBM per device.

v0:
```python
import jax
import jax.numpy as jnp
from jax import lax
from jax.sharding import PartitionSpec as P

NC_GRP = 8


def local(matrix, columns, counts, fine_guess, right_side, aggregate, restrict):
    column_vector = lax.all_gather(fine_guess, "row", axis=0, tiled=True)
    slot_count = matrix.shape[1]
    usable = jnp.arange(slot_count, dtype=jnp.int32)[None, :] < counts
    picked = jnp.take(column_vector, columns, axis=0) * usable[:, :, None, None].astype(jnp.float32)
    partial_value = jnp.einsum("gsab,gsvb->gva", matrix, picked, precision=lax.Precision.HIGHEST)
    product = lax.psum_scatter(partial_value, "col", scatter_dimension=0, tiled=True)
    residual = right_side - product
    contrib = jnp.einsum("gva,gak->gvk", residual, restrict, precision=lax.Precision.HIGHEST)
    onehot = (aggregate[:, None] == jnp.arange(NC_GRP, dtype=jnp.int32)[None, :]).astype(
        jnp.float32
    )
    coarse_part = jnp.einsum("gc,gvk->cvk", onehot, contrib, precision=lax.Precision.HIGHEST)
    squares = jnp.sum(residual * residual, axis=(0, 2))
    coarse = lax.psum(coarse_part, "col")
    total_sq = lax.psum(squares, ("row", "col"))
    entries = residual.shape[0] * residual.shape[2] * lax.axis_size("row") * lax.axis_size("col")
    scale_rms = jnp.sqrt(total_sq / entries + 1e-06)
    return (coarse / scale_rms[None, :, None], residual)


def solution(mesh):
    in_specs = (
        P("row", "col", None, None),
        P("row", "col"),
        P("row", "col"),
        P(("col", "row"), None, None),
        P(("row", "col"), None, None),
        P(("row", "col")),
        P(("row", "col"), None, None),
    )
    out_specs = (P("row", None, None), P(("row", "col"), None, None))
    return jax.shard_map(local, mesh=mesh, in_specs=in_specs, out_specs=out_specs, check_vma=False)
```

profile of v0, /device:TPU:0, one launch (start us, length us, event | category | flops | bytes accessed | tf_op | source)
XLA Modules:
  0.0 115.5 jit_solution(6656684423005813290)
XLA Ops:
  7.2 0.0 copy-start
  7.2 0.0 copy-start.4
  7.2 0.0 reduce-scatter.2.cloned.1.call-start
  7.2 0.8 compare_select_fusion
  8.0 0.0 copy-done.4
  8.0 32.8 %all_gather.3 = f32[16,32,128]{2,1,0:T(8,128)S(1)} all-gather(f32[2,32,128]{2,1,0:T(8,128)} %param.10), channel_id=1, replica_groups=mesh['row'=8,'col'=4] {'row'}, dimensions={0}, use_global_device_ids=true | all-gather | bytes 294912 | tf_op jit(solution)/shard_map/all_gather | solution.py:10
  40.8 0.1 copy.16
  40.9 0.1 reshape.37
  40.9 0.0 copy-start.6
  41.0 0.6 copy-done.6
  41.6 0.1 fusion.7
  41.7 0.1 copy.15
  41.8 0.6 gather_fusion
  42.3 0.0 copy-done
  42.4 0.0 copy-start.3
  42.4 1.9 %convolution_bitcast_fusion = f32[8,32,128]{2,1,0:T(8,128)} fusion(f32[8,2,128,128]{3,2,1,0:T(8,128)S(1)} %copy-done, f32[8,2,32,128]{3,2,1,0:T(8,128)S(1)} %bitcast.11, f32[8,2]{1,0:T(8,128)S(1)} %fusion.7, pred[8,2]{1,0:T(8,128)(4,1)S(1)} %copy.15), kind=kOutput, calls=%fused_computation.1 | convolution fusion | flops 100794368 | bytes 1441872 | tf_op jit(solution)/shard_map/gsab,gsvb->gva/dot_general | solution.py:14
  44.3 0.0 reduce-scatter.2.cloned.1.call-update
  44.3 0.0 all-reduce.2.cloned.1.call-start
  44.3 20.7 %reduce-scatter.2.cloned.1.call-done = f32[2,32,128]{2,1,0:T(8,128)} async-done(((f32[8,32,128]{2,1,0:T(8,128)}), f32[2,32,128]{2,1,0:T(8,128)}) %reduce-scatter.2.cloned.1.call-update) | async-done | bytes 32784 | tf_op jit(solution)/shard_map/reduce_scatter | solution.py:15
  65.0 0.0 copy-done.3
  65.0 0.9 multiply_reduce_fusion
  65.9 0.0 copy-done.1
  65.9 0.0 copy-start.5
  65.9 0.2 fusion.13
  66.2 0.4 copy-done.2
  66.5 0.1 copy-done.5
  66.6 1.0 fusion.5
  67.6 0.0 all-reduce.2.cloned.1.call-update
  67.6 39.3 %psum.15 = f32[32]{0:T(128)S(1)} all-reduce(f32[32]{0:T(128)S(1)} %get-tuple-element.8), channel_id=1, replica_groups=mesh['row'=8,'col'=4] {'row','col'}, use_global_device_ids=true, to_apply=%region_3.4 | all-reduce | flops 32 | bytes 256 | tf_op jit(solution)/shard_map/psum | solution.py:24
  106.9 0.0 all-reduce.2.cloned.1.call-done
  107.0 1.0 broadcast_divide_fusion
  108.0 0.7 copy.18
  (5 shorter events, 0.0 us)
Async XLA Ops:
  7.2 35.2 %copy-start = (f32[8,2,128,128]{3,2,1,0:T(8,128)S(1)}, f32[8,2,128,128]{3,2,1,0:T(8,128)}, u32[]{:S(2)}) copy-start(f32[8,2,128,128]{3,2,1,0:T(8,128)} %param.7) | copy-start | bytes 3145732
  7.2 0.8 copy-start.4
  7.2 57.8 %reduce-scatter.2.cloned.1.call-start = ((), (), s32[]{:S(2)}) async-start(), calls=%async_computation.1 | async-start | bytes 163840 | tf_op jit(solution)/shard_map/reduce_scatter | solution.py:15
  40.9 0.7 copy-start.6
  42.4 22.7 %copy-start.3 = (f32[2,32,128]{2,1,0:T(8,128)S(1)}, f32[2,32,128]{2,1,0:T(8,128)}, u32[]{:S(2)}) copy-start(f32[2,32,128]{2,1,0:T(8,128)} %param.11) | copy-start | bytes 98308
  44.3 21.7 %copy-start.1 = (f32[2,128,128]{2,1,0:T(8,128)S(1)}, f32[2,128,128]{2,1,0:T(8,128)}, u32[]{:S(2)}) copy-start(f32[2,128,128]{2,1,0:T(8,128)} %param.13) | copy-start | bytes 393220
  44.3 62.7 %all-reduce.2.cloned.1.call-start = ((), (), s32[]{:S(2)}) async-start(), calls=%async_computation.2 | async-start | bytes 262144 | tf_op jit(solution)/shard_map/psum | solution.py:23
  65.9 0.6 copy-start.2
  65.9 0.7 copy-start.5
Sparse Core Ops, SparseCore 0:
  44.4 20.5 reduce-scatter.1
  67.9 31.7 all-reduce.1
where the time goes:
time: 116 us; the launch traced here: 115 us
  blocking collectives  72.1 us (62%)
  waiting for transfers between devices  20.8 us (18%)
  between operations  14.1 us (12%)
  matrix products  3.07 us (3%)
  other arithmetic  2.73 us (2%)
  local copies, waits for them, and re-layouts  2.62 us (2%)
    psum x1, blocking collectives, local(): total_sq = lax.psum(squares, ('row', 'col'))  39.3 us
    all_gather x1, blocking collectives, local(): column_vector = lax.all_gather(fine_guess, 'row', axis=0, tiled=True)  32.8 us
    reduce_scatter x1, waiting for transfers between devices, local(): lax.psum_scatter(partial_value, 'col', scatter_dimension=0, tiled=True)  20.7 us
  transfers between devices with their start and end apart: 2, of which 1 were waited for; matrix products, arithmetic and copies ran while one was open for 0% of the time, Pallas kernels for 0%

commit v1 on v0

--- a/solution.py
+++ b/solution.py
@@ -21,7 +21,7 @@
     coarse_part = jnp.einsum("gc,gvk->cvk", onehot, contrib, precision=lax.Precision.HIGHEST)
     squares = jnp.sum(residual * residual, axis=(0, 2))
     coarse = lax.psum(coarse_part, "col")
-    total_sq = lax.psum(squares, ("row", "col"))
+    total_sq = jnp.sum(lax.all_gather(squares, ("row", "col")), axis=0)
     entries = residual.shape[0] * residual.shape[2] * lax.axis_size("row") * lax.axis_size("col")
     scale_rms = jnp.sqrt(total_sq / entries + 1e-06)
     return (coarse / scale_rms[None, :, None], residual)

time: 116 us -> 116 us (level)
    psum x1 -> x0, blocking collectives: 39.3 us -> none  [local(): total_sq = lax.psum(squares, ('row', 'col'))]
    unnamed x0 -> x1, blocking collectives: none -> 39.3 us
where the time goes in v1:
time: 116 us
  blocking collectives  72.1 us (62%)
  waiting for transfers between devices  20.7 us (18%)
  between operations  14.1 us (12%)
  matrix products  3.07 us (3%)
  local copies, waits for them, and re-layouts  2.94 us (3%)
  other arithmetic  2.76 us (2%)
    unnamed x1, blocking collectives  39.3 us
    all_gather x1, blocking collectives, local(): column_vector = lax.all_gather(fine_guess, 'row', axis=0, tiled=True)  32.8 us
    reduce_scatter x1, waiting for transfers between devices, local(): lax.psum_scatter(partial_value, 'col', scatter_dimension=0, tiled=True)  20.7 us
  transfers between devices with their start and end apart: 2, of which 1 were waited for; matrix products, arithmetic and copies ran while one was open for 0% of the time, Pallas kernels for 0%

profile of v1, /device:TPU:0, one launch (start us, length us, event | category | flops | bytes accessed | tf_op | source)
XLA Modules:
  0.0 115.8 jit_solution(1562504987354502267)
XLA Ops:
  7.2 0.0 copy-start
  7.2 0.0 copy-start.4
  7.2 0.0 reduce-scatter.2.cloned.1.call-start
  7.2 0.8 compare_select_fusion
  8.0 0.0 copy-done.4
  8.0 32.8 %all_gather.9 = f32[16,32,128]{2,1,0:T(8,128)S(1)} all-gather(f32[2,32,128]{2,1,0:T(8,128)} %param.10), channel_id=1, replica_groups=mesh['row'=8,'col'=4] {'row'}, dimensions={0}, use_global_device_ids=true | all-gather | bytes 294912 | tf_op jit(solution)/shard_map/all_gather | solution.py:10
  40.8 0.1 copy.20
  40.9 0.1 reshape.41
  40.9 0.0 copy-start.6
  41.0 0.6 copy-done.6
  41.6 0.1 fusion.7
  41.7 0.1 copy.19
  41.8 0.6 gather_fusion
  42.3 0.0 copy-done
  42.4 0.0 copy-start.3
  42.4 1.9 %convolution_bitcast_fusion = f32[8,32,128]{2,1,0:T(8,128)} fusion(f32[8,2,128,128]{3,2,1,0:T(8,128)S(1)} %copy-done, f32[8,2,32,128]{3,2,1,0:T(8,128)S(1)} %bitcast.11, f32[8,2]{1,0:T(8,128)S(1)} %fusion.7, pred[8,2]{1,0:T(8,128)(4,1)S(1)} %copy.19), kind=kOutput, calls=%fused_computation.1 | convolution fusion | flops 100794368 | bytes 1441872 | tf_op jit(solution)/shard_map/gsab,gsvb->gva/dot_general | solution.py:14
  44.3 0.0 reduce-scatter.2.cloned.1.call-update
  44.3 0.0 all-reduce.3.cloned.1.call-start
  44.3 20.7 %reduce-scatter.2.cloned.1.call-done = f32[2,32,128]{2,1,0:T(8,128)} async-done(((f32[8,32,128]{2,1,0:T(8,128)}), f32[2,32,128]{2,1,0:T(8,128)}) %reduce-scatter.2.cloned.1.call-update) | async-done | bytes 32784 | tf_op jit(solution)/shard_map/reduce_scatter | solution.py:15
  65.0 0.9 multiply_reduce_fusion
  65.9 0.0 copy-start.5
  65.9 0.2 fusion.13
  66.2 0.4 copy-done.2
  66.5 0.1 copy-done.5
  66.6 1.0 fusion.5
  67.6 0.0 all-reduce.3.cloned.1.call-update
  67.6 0.2 dynamic-update-slice
  67.8 39.3 %all-reduce = f32[1024]{0:T(1024)S(1)} all-reduce(f32[1024]{0:T(1024)S(1)} %dynamic-update-slice), channel_id=2, replica_groups=mesh['row'=8,'col'=4] {'row','col'}, use_global_device_ids=true, to_apply=%add | all-reduce | flops 1024 | bytes 8192
  107.2 0.1 reshape.47
  107.3 0.0 all-reduce.3.cloned.1.call-done
  107.3 1.0 broadcast_divide_fusion
  108.3 0.7 copy.22
  (9 shorter events, 0.1 us)
Async XLA Ops:
  7.2 35.2 %copy-start = (f32[8,2,128,128]{3,2,1,0:T(8,128)S(1)}, f32[8,2,128,128]{3,2,1,0:T(8,128)}, u32[]{:S(2)}) copy-start(f32[8,2,128,128]{3,2,1,0:T(8,128)} %param.7) | copy-start | bytes 3145732
  7.2 0.8 copy-start.4
  7.2 57.8 %reduce-scatter.2.cloned.1.call-start = ((), (), s32[]{:S(2)}) async-start(), calls=%async_computation.1 | async-start | bytes 163840 | tf_op jit(solution)/shard_map/reduce_scatter | solution.py:15
  40.9 0.7 copy-start.6
  42.4 22.7 %copy-start.3 = (f32[2,32,128]{2,1,0:T(8,128)S(1)}, f32[2,32,128]{2,1,0:T(8,128)}, u32[]{:S(2)}) copy-start(f32[2,32,128]{2,1,0:T(8,128)} %param.11) | copy-start | bytes 98308
  44.3 21.7 %copy-start.1 = (f32[2,128,128]{2,1,0:T(8,128)S(1)}, f32[2,128,128]{2,1,0:T(8,128)}, u32[]{:S(2)}) copy-start(f32[2,128,128]{2,1,0:T(8,128)} %param.13) | copy-start | bytes 393220
  44.3 63.0 %all-reduce.3.cloned.1.call-start = ((), (), s32[]{:S(2)}) async-start(), calls=%async_computation.2 | async-start | bytes 262144 | tf_op jit(solution)/shard_map/psum | solution.py:23
  65.9 0.6 copy-start.2
  65.9 0.7 copy-start.5
Sparse Core Ops, SparseCore 0:
  44.4 20.5 reduce-scatter.1
  67.9 31.7 all-reduce.2
